TPU v7x, 64 devices: a 2x2x8 block of a 4x4x8 slice. The times are simulated.
64 devices in a mesh: data: 4 (over x, y), ctx: 16 (over z, core).
Axes of the slice: x: 2, y: 2, z: 8, core: 2. Of those that a mesh axis runs over, the one named last changes fastest.
The devices are a block of a 4x4x8 slice.
Arguments:
- queries: bfloat16 [4, 32768, 2, 256], P('data', 'ctx'), parts along dimension 0
- key_rows: bfloat16 [4, 32768, 1, 256], P('data', 'ctx'), parts along dimension 0
- value_rows: bfloat16 [4, 32768, 1, 256], P('data', 'ctx'), parts along dimension 0
Outputs:
- output: bfloat16 [4, 32768, 2, 256], P('data', 'ctx'), parts along dimension 0
There are 4 independent parts. A program takes and returns all parts, laid end to end along the dimension named above; each array names one.
All inputs are finite; a program needn't handle non-finite values.
Results may differ from a plain program's by a relative error of at most 0.00204687.
Values are sent between devices in bfloat16 or wider.
A program may use at most 768 MiB of HBM per device.

v0:
```python
import math
import jax
import jax.numpy as jnp
from jax import lax
from jax.sharding import PartitionSpec as P


def solution(mesh):
    groups = mesh.shape["ctx"]
    rounds = groups // 2
    next_perm = [(src, (src + 1) % groups) for src in range(groups)]
    home_perm = [(src, (src - rounds) % groups) for src in range(groups)]
    seq_spec = P("data", "ctx", None, None)

    def local_attention(queries, key_rows, value_rows):
        n_batch, chunk_len, n_heads, head_dim = queries.shape
        kv_heads = key_rows.shape[2]
        group_ratio = n_heads // kv_heads
        score_scale = 1.0 / math.sqrt(head_dim)
        my_index = lax.axis_index("ctx")
        q_local = queries.reshape(n_batch, chunk_len, kv_heads, group_ratio, head_dim)

        def empty_acc():
            return (
                jnp.zeros((n_batch, chunk_len, kv_heads, group_ratio, head_dim), jnp.float32),
                jnp.full((n_batch, kv_heads, group_ratio, chunk_len), -jnp.inf, jnp.float32),
                jnp.zeros((n_batch, kv_heads, group_ratio, chunk_len), jnp.float32),
            )

        def to_rows(stat):
            return jnp.transpose(stat, (0, 3, 1, 2))[..., None]

        def attend(acc_in, q_blk, k_blk, v_blk, masked):
            key_len = k_blk.shape[1]
            tile_len = min(key_len, 256)
            row_pos = jnp.arange(q_blk.shape[1])[:, None]

            def tile_update(tile_idx, acc_now):
                o_acc, m_acc, l_acc = acc_now
                k_tile = lax.dynamic_slice_in_dim(k_blk, tile_idx * tile_len, tile_len, axis=1)
                v_tile = lax.dynamic_slice_in_dim(v_blk, tile_idx * tile_len, tile_len, axis=1)
                scores = jnp.einsum("bqhgd,bkhd->bhgqk", q_blk, k_tile,
                                    preferred_element_type=jnp.float32) * score_scale
                if masked:
                    col_pos = tile_idx * tile_len + jnp.arange(tile_len)[None, :]
                    scores = jnp.where(row_pos >= col_pos, scores, -jnp.inf)
                m_new = jnp.maximum(m_acc, jnp.max(scores, axis=-1))
                rescale = jnp.exp(m_acc - m_new)
                exp_scores = jnp.exp(scores - m_new[..., None])
                l_new = l_acc * rescale + jnp.sum(exp_scores, axis=-1)
                pv_part = jnp.einsum("bhgqk,bkhd->bqhgd", exp_scores.astype(jnp.bfloat16), v_tile,
                                     preferred_element_type=jnp.float32)
                return (o_acc * to_rows(rescale) + pv_part, m_new, l_new)

            return lax.fori_loop(0, key_len // tile_len, tile_update, acc_in)

        acc_first = attend(empty_acc(), q_local, key_rows, value_rows, True)

        def round_body(round_idx, loop_state):
            kv_trav, q_trav, acc_local, acc_trav = loop_state
            kv_trav = lax.ppermute(kv_trav, "ctx", next_perm)
            q_trav = lax.ppermute(q_trav, "ctx", next_perm)
            acc_trav = lax.ppermute(acc_trav, "ctx", next_perm)
            choice = jnp.where(my_index >= round_idx, 0, jnp.where(2 * round_idx < groups, 1, 2))

            def own_queries(acc_pair):
                return (attend(acc_pair[0], q_local, kv_trav[0], kv_trav[1], False), acc_pair[1])

            def visiting_queries(acc_pair):
                return (acc_pair[0], attend(acc_pair[1], q_trav, key_rows, value_rows, False))

            def no_work(acc_pair):
                return acc_pair

            acc_local, acc_trav = lax.switch(choice, [own_queries, visiting_queries, no_work],
                                             (acc_local, acc_trav))
            return (kv_trav, q_trav, acc_local, acc_trav)

        loop_state = lax.fori_loop(1, rounds + 1, round_body,
                                   ((key_rows, value_rows), q_local, acc_first, empty_acc()))
        acc_home = lax.ppermute(loop_state[3], "ctx", home_perm)
        o_loc, m_loc, l_loc = loop_state[2]
        o_far, m_far, l_far = acc_home
        m_both = jnp.maximum(m_loc, m_far)
        w_loc = jnp.exp(m_loc - m_both)
        w_far = jnp.exp(m_far - m_both)
        denominator = l_loc * w_loc + l_far * w_far
        numerator = o_loc * to_rows(w_loc) + o_far * to_rows(w_far)
        out_rows = numerator / to_rows(denominator)
        return out_rows.astype(jnp.bfloat16).reshape(n_batch, chunk_len, n_heads, head_dim)

    return jax.shard_map(local_attention, mesh=mesh, in_specs=(seq_spec, seq_spec, seq_spec),
                         out_specs=seq_spec, check_vma=False)
```

profile of v0, /device:TPU:61, one launch (start us, length us, event | category | flops | bytes accessed | tf_op | source)
XLA Modules:
  0.0 1698.4 jit_solution(14574883862383796790)
XLA Ops:
  4.2 14.0 copy.30
  20.4 103.9 %while.82 = (s32[]{:T(128)}, f32[1,2048,1,2,256]{1,4,3,2,0:T(8,128)}, f32[1,1,2,2048]{3,2,1,0:T(2,128)S(1)}, f32[1,1,2,2048]{3,2,1,0:T(2,128)S(1)}, bf16[1,2048,...) while((s32[]{:T(128)}, ...), condition=%wide.region_3.4_spmd.clone, body=%wide.region_0.3_spmd.clone.sunk | while | flops 1084776704 | bytes 41421004 | solution.py:55
  127.2 1333.1 %while.81 = (s32[]{:T(128)}, bf16[1,2048,1,256]{3,1,2,0:T(8,128)(2,1)}, bf16[1,2048,1,256]{1,3,2,0:T(8,128)(2,1)}, bf16[1,2048,1,2,256]{4,3,2,1,0:T(2,128)(2,1)}...) while((s32[]{:T(128)}, ...), condition=%wide.region_16.17_spmd, body=%wide.region_4.16_spmd.sunk | while | flops 1084239872 | bytes 145425472 | solution.py:79
  135.5 73.5 %collective-permute-done = bf16[1,2048,1,256]{3,1,2,0:T(8,128)(2,1)} collective-permute-done((bf16[1,2048,1,256]{3,1,2,0:T(8,128)(2,1)}, bf16[1,2048,1,256]{3,1,2,0:T(8,128)(2,1)}, u32[]{:S(2)}, u32[]{:S(2)}) %collective-permute-start) | collective-permute-done | bytes 1048608 | tf_op jit(solution)/shard_map/while/body/eval_jaxpr/ppermute | solution.py:61
  213.8 6.4 collective-permute-done.1
  225.6 63.2 %conditional.2 = ((f32[1,2048,1,2,256]{1,4,3,2,0:T(8,128)}, f32[1,1,2,2048]{3,2,1,0:T(2,128)S(1)}, f32[1,1,2,2048]{3,2,1,0:T(2,128)S(1)}, f32[1,2048,1,2,256]{4,...) conditional(s32[]{:T(128)} %clamp.8, ...), branch_computations={%region_5.9_spmd, %region_10.14_spmd, %region_15.15_spmd} | conditional | flops 1084239872 | bytes 78119280 | solution.py:75
  225.6 63.2 %while.79 = (s32[]{:T(128)}, f32[1,2048,1,2,256]{1,4,3,2,0:T(8,128)}, f32[1,1,2,2048]{3,2,1,0:T(2,128)S(1)}, f32[1,1,2,2048]{3,2,1,0:T(2,128)S(1)}, bf16[1,2048,...) while((s32[]{:T(128)}, ...), condition=%wide.region_9.8_spmd, body=%wide.region_6.7_spmd.sunk | while | flops 1084239872 | bytes 23593124 | solution.py:55
  288.8 5.5 copy.123
  303.8 72.2 %collective-permute-done = bf16[1,2048,1,256]{3,1,2,0:T(8,128)(2,1)} collective-permute-done((bf16[1,2048,1,256]{3,1,2,0:T(8,128)(2,1)}, bf16[1,2048,1,256]{3,1,2,0:T(8,128)(2,1)}, u32[]{:S(2)}, u32[]{:S(2)}) %collective-permute-start) | collective-permute-done | bytes 1048608 | tf_op jit(solution)/shard_map/while/body/eval_jaxpr/ppermute | solution.py:61
  380.8 6.4 collective-permute-done.1
  392.7 63.2 %conditional.2 = ((f32[1,2048,1,2,256]{1,4,3,2,0:T(8,128)}, f32[1,1,2,2048]{3,2,1,0:T(2,128)S(1)}, f32[1,1,2,2048]{3,2,1,0:T(2,128)S(1)}, f32[1,2048,1,2,256]{4,...) conditional(s32[]{:T(128)} %clamp.8, ...), branch_computations={%region_5.9_spmd, %region_10.14_spmd, %region_15.15_spmd} | conditional | flops 1084239872 | bytes 78119280 | solution.py:75
  392.7 63.2 %while.79 = (s32[]{:T(128)}, f32[1,2048,1,2,256]{1,4,3,2,0:T(8,128)}, f32[1,1,2,2048]{3,2,1,0:T(2,128)S(1)}, f32[1,1,2,2048]{3,2,1,0:T(2,128)S(1)}, bf16[1,2048,...) while((s32[]{:T(128)}, ...), condition=%wide.region_9.8_spmd, body=%wide.region_6.7_spmd.sunk | while | flops 1084239872 | bytes 23593124 | solution.py:55
  472.0 71.0 %collective-permute-done = bf16[1,2048,1,256]{3,1,2,0:T(8,128)(2,1)} collective-permute-done((bf16[1,2048,1,256]{3,1,2,0:T(8,128)(2,1)}, bf16[1,2048,1,256]{3,1,2,0:T(8,128)(2,1)}, u32[]{:S(2)}, u32[]{:S(2)}) %collective-permute-start) | collective-permute-done | bytes 1048608 | tf_op jit(solution)/shard_map/while/body/eval_jaxpr/ppermute | solution.py:61
  547.9 6.4 collective-permute-done.1
  559.8 63.2 %conditional.2 = ((f32[1,2048,1,2,256]{1,4,3,2,0:T(8,128)}, f32[1,1,2,2048]{3,2,1,0:T(2,128)S(1)}, f32[1,1,2,2048]{3,2,1,0:T(2,128)S(1)}, f32[1,2048,1,2,256]{4,...) conditional(s32[]{:T(128)} %clamp.8, ...), branch_computations={%region_5.9_spmd, %region_10.14_spmd, %region_15.15_spmd} | conditional | flops 1084239872 | bytes 78119280 | solution.py:75
  559.8 63.2 %while.79 = (s32[]{:T(128)}, f32[1,2048,1,2,256]{1,4,3,2,0:T(8,128)}, f32[1,1,2,2048]{3,2,1,0:T(2,128)S(1)}, f32[1,1,2,2048]{3,2,1,0:T(2,128)S(1)}, bf16[1,2048,...) while((s32[]{:T(128)}, ...), condition=%wide.region_9.8_spmd, body=%wide.region_6.7_spmd.sunk | while | flops 1084239872 | bytes 23593124 | solution.py:55
  640.3 69.8 %collective-permute-done = bf16[1,2048,1,256]{3,1,2,0:T(8,128)(2,1)} collective-permute-done((bf16[1,2048,1,256]{3,1,2,0:T(8,128)(2,1)}, bf16[1,2048,1,256]{3,1,2,0:T(8,128)(2,1)}, u32[]{:S(2)}, u32[]{:S(2)}) %collective-permute-start) | collective-permute-done | bytes 1048608 | tf_op jit(solution)/shard_map/while/body/eval_jaxpr/ppermute | solution.py:61
  715.0 6.4 collective-permute-done.1
  726.8 9.0 collective-permute-done.5
  735.8 74.7 %conditional.2 = ((f32[1,2048,1,2,256]{1,4,3,2,0:T(8,128)}, f32[1,1,2,2048]{3,2,1,0:T(2,128)S(1)}, f32[1,1,2,2048]{3,2,1,0:T(2,128)S(1)}, f32[1,2048,1,2,256]{4,...) conditional(s32[]{:T(128)} %clamp.8, ...), branch_computations={%region_5.9_spmd, %region_10.14_spmd, %region_15.15_spmd} | conditional | flops 1084239872 | bytes 78119280 | solution.py:75
  735.8 7.4 copy.25
  745.0 58.2 %while.80 = (s32[]{:T(128)}, f32[1,2048,1,2,256]{1,4,3,2,0:T(8,128)}, f32[1,1,2,2048]{3,2,1,0:T(2,128)S(1)}, f32[1,1,2,2048]{3,2,1,0:T(2,128)S(1)}, bf16[1,2048,...) while((s32[]{:T(128)}, ...), condition=%wide.region_14.13_spmd, body=%wide.region_11.12_spmd.sunk | while | flops 1084239872 | bytes 57147608 | solution.py:55
  803.2 7.2 copy.22
  816.3 78.8 %collective-permute-done = bf16[1,2048,1,256]{3,1,2,0:T(8,128)(2,1)} collective-permute-done((bf16[1,2048,1,256]{3,1,2,0:T(8,128)(2,1)}, bf16[1,2048,1,256]{3,1,2,0:T(8,128)(2,1)}, u32[]{:S(2)}, u32[]{:S(2)}) %collective-permute-start) | collective-permute-done | bytes 1048608 | tf_op jit(solution)/shard_map/while/body/eval_jaxpr/ppermute | solution.py:61
  900.0 6.4 collective-permute-done.1
  915.6 74.7 %conditional.2 = ((f32[1,2048,1,2,256]{1,4,3,2,0:T(8,128)}, f32[1,1,2,2048]{3,2,1,0:T(2,128)S(1)}, f32[1,1,2,2048]{3,2,1,0:T(2,128)S(1)}, f32[1,2048,1,2,256]{4,...) conditional(s32[]{:T(128)} %clamp.8, ...), branch_computations={%region_5.9_spmd, %region_10.14_spmd, %region_15.15_spmd} | conditional | flops 1084239872 | bytes 78119280 | solution.py:75
  915.6 7.4 copy.25
  924.8 58.2 %while.80 = (s32[]{:T(128)}, f32[1,2048,1,2,256]{1,4,3,2,0:T(8,128)}, f32[1,1,2,2048]{3,2,1,0:T(2,128)S(1)}, f32[1,1,2,2048]{3,2,1,0:T(2,128)S(1)}, bf16[1,2048,...) while((s32[]{:T(128)}, ...), condition=%wide.region_14.13_spmd, body=%wide.region_11.12_spmd.sunk | while | flops 1084239872 | bytes 57147608 | solution.py:55
  983.0 7.2 copy.22
  996.1 78.8 %collective-permute-done = bf16[1,2048,1,256]{3,1,2,0:T(8,128)(2,1)} collective-permute-done((bf16[1,2048,1,256]{3,1,2,0:T(8,128)(2,1)}, bf16[1,2048,1,256]{3,1,2,0:T(8,128)(2,1)}, u32[]{:S(2)}, u32[]{:S(2)}) %collective-permute-start) | collective-permute-done | bytes 1048608 | tf_op jit(solution)/shard_map/while/body/eval_jaxpr/ppermute | solution.py:61
  1079.7 6.4 collective-permute-done.1
  1095.3 74.7 %conditional.2 = ((f32[1,2048,1,2,256]{1,4,3,2,0:T(8,128)}, f32[1,1,2,2048]{3,2,1,0:T(2,128)S(1)}, f32[1,1,2,2048]{3,2,1,0:T(2,128)S(1)}, f32[1,2048,1,2,256]{4,...) conditional(s32[]{:T(128)} %clamp.8, ...), branch_computations={%region_5.9_spmd, %region_10.14_spmd, %region_15.15_spmd} | conditional | flops 1084239872 | bytes 78119280 | solution.py:75
  1095.3 7.4 copy.25
  1104.6 58.2 %while.80 = (s32[]{:T(128)}, f32[1,2048,1,2,256]{1,4,3,2,0:T(8,128)}, f32[1,1,2,2048]{3,2,1,0:T(2,128)S(1)}, f32[1,1,2,2048]{3,2,1,0:T(2,128)S(1)}, bf16[1,2048,...) while((s32[]{:T(128)}, ...), condition=%wide.region_14.13_spmd, body=%wide.region_11.12_spmd.sunk | while | flops 1084239872 | bytes 57147608 | solution.py:55
  1162.7 7.2 copy.22
  1175.8 78.8 %collective-permute-done = bf16[1,2048,1,256]{3,1,2,0:T(8,128)(2,1)} collective-permute-done((bf16[1,2048,1,256]{3,1,2,0:T(8,128)(2,1)}, bf16[1,2048,1,256]{3,1,2,0:T(8,128)(2,1)}, u32[]{:S(2)}, u32[]{:S(2)}) %collective-permute-start) | collective-permute-done | bytes 1048608 | tf_op jit(solution)/shard_map/while/body/eval_jaxpr/ppermute | solution.py:61
  1259.5 6.4 collective-permute-done.1
  1275.1 74.7 %conditional.2 = ((f32[1,2048,1,2,256]{1,4,3,2,0:T(8,128)}, f32[1,1,2,2048]{3,2,1,0:T(2,128)S(1)}, f32[1,1,2,2048]{3,2,1,0:T(2,128)S(1)}, f32[1,2048,1,2,256]{4,...) conditional(s32[]{:T(128)} %clamp.8, ...), branch_computations={%region_5.9_spmd, %region_10.14_spmd, %region_15.15_spmd} | conditional | flops 1084239872 | bytes 78119280 | solution.py:75
  1275.1 7.4 copy.25
  1284.3 58.2 %while.80 = (s32[]{:T(128)}, f32[1,2048,1,2,256]{1,4,3,2,0:T(8,128)}, f32[1,1,2,2048]{3,2,1,0:T(2,128)S(1)}, f32[1,1,2,2048]{3,2,1,0:T(2,128)S(1)}, bf16[1,2048,...) while((s32[]{:T(128)}, ...), condition=%wide.region_14.13_spmd, body=%wide.region_11.12_spmd.sunk | while | flops 1084239872 | bytes 57147608 | solution.py:55
  1342.5 7.2 copy.22
  1355.6 78.8 %collective-permute-done = bf16[1,2048,1,256]{3,1,2,0:T(8,128)(2,1)} collective-permute-done((bf16[1,2048,1,256]{3,1,2,0:T(8,128)(2,1)}, bf16[1,2048,1,256]{3,1,2,0:T(8,128)(2,1)}, u32[]{:S(2)}, u32[]{:S(2)}) %collective-permute-start) | collective-permute-done | bytes 1048608 | tf_op jit(solution)/shard_map/while/body/eval_jaxpr/ppermute | solution.py:61
  1439.2 6.4 collective-permute-done.1
  1454.8 5.5 copy.123
  1460.3 51.3 %collective-permute-start.7 = (f32[1,2048,1,2,256]{4,3,1,2,0:T(2,128)}, f32[1,2048,1,2,256]{4,3,1,2,0:T(2,128)}, u32[]{:S(2)}, u32[]{:S(2)}) collective-permute-start(f32[1,2048,1,2,256]{4,3,1,2,0:T(2,128)} %bitcast.221), channel_id=1, source_target_pairs={{0,8},{1,9},{2,10},{3,11},{4,12},{5,13},{6,14},{7,15},{8,0},{9,1},... | collective-permute-start | bytes 12582920 | tf_op jit(solution)/shard_map/ppermute | solution.py:81
  1517.0 7.2 copy.32
  1524.3 163.1 %collective-permute-done.6 = f32[1,1,2,2048]{3,2,1,0:T(2,128)S(1)} collective-permute-done((f32[1,1,2,2048]{3,2,1,0:T(2,128)S(1)}, f32[1,1,2,2048]{3,2,1,0:T(2,128)S(1)}, u32[]{:S(2)}, u32[]{:S(2)}) %collective-permute-start.6) | collective-permute-done | bytes 16416 | tf_op jit(solution)/shard_map/ppermute | solution.py:81
  1688.7 9.6 fusion.50
  (723 shorter events, 718.5 us)
Async XLA Ops:
  127.5 98.2 %collective-permute-start.3 = (f32[1,2048,1,2,256]{4,3,2,1,0:T(2,128)}, f32[1,2048,1,2,256]{4,3,2,1,0:T(2,128)}, u32[]{:S(2)}, u32[]{:S(2)}) collective-permute-start(f32[1,2048,1,2,256]{4,3,2,1,0:T(2,128)} %get-tuple-element.1300), channel_id=1, source_target_pairs={{0,1},{1,2},{2,3},{3,4},{4,5},{5,6},{6,7},{7,8},{8,9},{9,10},{10,1... | collective-permute-start | bytes 12582920 | tf_op jit(solution)/shard_map/while/body/eval_jaxpr/ppermute | solution.py:63
  129.8 91.4 %collective-permute-start.2 = (bf16[1,2048,1,2,256]{4,3,2,1,0:T(2,128)(2,1)}, bf16[1,2048,1,2,256]{4,3,2,1,0:T(2,128)(2,1)}, u32[]{:S(2)}, u32[]{:S(2)}) collective-permute-start(bf16[1,2048,1,2,256]{4,3,2,1,0:T(2,128)(2,1)} %get-tuple-element.1296), channel_id=1, source_target_pairs={{0,1},{1,2},{2,3},{3,4},{4,5},{5,6},{6,7},{7,8},{8,9},{9,10},{10,1... | collective-permute-start | bytes 6291464 | tf_op jit(solution)/shard_map/while/body/eval_jaxpr/ppermute | solution.py:62
  129.9 79.1 %collective-permute-start = (bf16[1,2048,1,256]{3,1,2,0:T(8,128)(2,1)}, bf16[1,2048,1,256]{3,1,2,0:T(8,128)(2,1)}, u32[]{:S(2)}, u32[]{:S(2)}) collective-permute-start(bf16[1,2048,1,256]{3,1,2,0:T(8,128)(2,1)} %get-tuple-element.1294), channel_id=1, source_target_pairs={{0,1},{1,2},{2,3},{3,4},{4,5},{5,6},{6,7},{7,8},{8,9},{9,10},{10,1... | collective-permute-start | bytes 3145736 | tf_op jit(solution)/shard_map/while/body/eval_jaxpr/ppermute | solution.py:61
  132.1 88.1 %collective-permute-start.1 = (bf16[1,2048,1,256]{1,3,2,0:T(8,128)(2,1)}, bf16[1,2048,1,256]{1,3,2,0:T(8,128)(2,1)S(1)}, u32[]{:S(2)}, u32[]{:S(2)}) collective-permute-start(bf16[1,2048,1,256]{1,3,2,0:T(8,128)(2,1)} %get-tuple-element.1295), channel_id=1, source_target_pairs={{0,1},{1,2},{2,3},{3,4},{4,5},{5,6},{6,7},{7,8},{8,9},{9,10},{10,1... | collective-permute-start | bytes 3145736 | tf_op jit(solution)/shard_map/while/body/eval_jaxpr/ppermute | solution.py:61
  132.1 93.5 %collective-permute-start.4 = (f32[1,1,2,2048]{3,2,1,0:T(2,128)S(1)}, f32[1,1,2,2048]{3,2,1,0:T(2,128)S(1)}, u32[]{:S(2)}, u32[]{:S(2)}) collective-permute-start(f32[1,1,2,2048]{3,2,1,0:T(2,128)S(1)} %get-tuple-element.1301), channel_id=1, source_target_pairs={{0,1},{1,2},{2,3},{3,4},{4,5},{5,6},{6,7},{7,8},{8,9},{9,10},{10,1... | collective-permute-start | bytes 49160 | tf_op jit(solution)/shard_map/while/body/eval_jaxpr/ppermute | solution.py:63
  294.3 98.4 %collective-permute-start.3 = (f32[1,2048,1,2,256]{4,3,2,1,0:T(2,128)}, f32[1,2048,1,2,256]{4,3,2,1,0:T(2,128)}, u32[]{:S(2)}, u32[]{:S(2)}) collective-permute-start(f32[1,2048,1,2,256]{4,3,2,1,0:T(2,128)} %get-tuple-element.1300), channel_id=1, source_target_pairs={{0,1},{1,2},{2,3},{3,4},{4,5},{5,6},{6,7},{7,8},{8,9},{9,10},{10,1... | collective-permute-start | bytes 12582920 | tf_op jit(solution)/shard_map/while/body/eval_jaxpr/ppermute | solution.py:63
  296.9 91.4 %collective-permute-start.2 = (bf16[1,2048,1,2,256]{4,3,2,1,0:T(2,128)(2,1)}, bf16[1,2048,1,2,256]{4,3,2,1,0:T(2,128)(2,1)}, u32[]{:S(2)}, u32[]{:S(2)}) collective-permute-start(bf16[1,2048,1,2,256]{4,3,2,1,0:T(2,128)(2,1)} %get-tuple-element.1296), channel_id=1, source_target_pairs={{0,1},{1,2},{2,3},{3,4},{4,5},{5,6},{6,7},{7,8},{8,9},{9,10},{10,1... | collective-permute-start | bytes 6291464 | tf_op jit(solution)/shard_map/while/body/eval_jaxpr/ppermute | solution.py:62
  297.0 79.1 %collective-permute-start = (bf16[1,2048,1,256]{3,1,2,0:T(8,128)(2,1)}, bf16[1,2048,1,256]{3,1,2,0:T(8,128)(2,1)}, u32[]{:S(2)}, u32[]{:S(2)}) collective-permute-start(bf16[1,2048,1,256]{3,1,2,0:T(8,128)(2,1)} %get-tuple-element.1294), channel_id=1, source_target_pairs={{0,1},{1,2},{2,3},{3,4},{4,5},{5,6},{6,7},{7,8},{8,9},{9,10},{10,1... | collective-permute-start | bytes 3145736 | tf_op jit(solution)/shard_map/while/body/eval_jaxpr/ppermute | solution.py:61
  299.1 88.1 %collective-permute-start.1 = (bf16[1,2048,1,256]{1,3,2,0:T(8,128)(2,1)}, bf16[1,2048,1,256]{1,3,2,0:T(8,128)(2,1)S(1)}, u32[]{:S(2)}, u32[]{:S(2)}) collective-permute-start(bf16[1,2048,1,256]{1,3,2,0:T(8,128)(2,1)} %get-tuple-element.1295), channel_id=1, source_target_pairs={{0,1},{1,2},{2,3},{3,4},{4,5},{5,6},{6,7},{7,8},{8,9},{9,10},{10,1... | collective-permute-start | bytes 3145736 | tf_op jit(solution)/shard_map/while/body/eval_jaxpr/ppermute | solution.py:61
  300.1 92.6 %collective-permute-start.4 = (f32[1,1,2,2048]{3,2,1,0:T(2,128)S(1)}, f32[1,1,2,2048]{3,2,1,0:T(2,128)S(1)}, u32[]{:S(2)}, u32[]{:S(2)}) collective-permute-start(f32[1,1,2,2048]{3,2,1,0:T(2,128)S(1)} %get-tuple-element.1301), channel_id=1, source_target_pairs={{0,1},{1,2},{2,3},{3,4},{4,5},{5,6},{6,7},{7,8},{8,9},{9,10},{10,1... | collective-permute-start | bytes 49160 | tf_op jit(solution)/shard_map/while/body/eval_jaxpr/ppermute | solution.py:63
  461.4 98.4 %collective-permute-start.3 = (f32[1,2048,1,2,256]{4,3,2,1,0:T(2,128)}, f32[1,2048,1,2,256]{4,3,2,1,0:T(2,128)}, u32[]{:S(2)}, u32[]{:S(2)}) collective-permute-start(f32[1,2048,1,2,256]{4,3,2,1,0:T(2,128)} %get-tuple-element.1300), channel_id=1, source_target_pairs={{0,1},{1,2},{2,3},{3,4},{4,5},{5,6},{6,7},{7,8},{8,9},{9,10},{10,1... | collective-permute-start | bytes 12582920 | tf_op jit(solution)/shard_map/while/body/eval_jaxpr/ppermute | solution.py:63
  464.0 91.4 %collective-permute-start.2 = (bf16[1,2048,1,2,256]{4,3,2,1,0:T(2,128)(2,1)}, bf16[1,2048,1,2,256]{4,3,2,1,0:T(2,128)(2,1)}, u32[]{:S(2)}, u32[]{:S(2)}) collective-permute-start(bf16[1,2048,1,2,256]{4,3,2,1,0:T(2,128)(2,1)} %get-tuple-element.1296), channel_id=1, source_target_pairs={{0,1},{1,2},{2,3},{3,4},{4,5},{5,6},{6,7},{7,8},{8,9},{9,10},{10,1... | collective-permute-start | bytes 6291464 | tf_op jit(solution)/shard_map/while/body/eval_jaxpr/ppermute | solution.py:62
  464.0 79.1 %collective-permute-start = (bf16[1,2048,1,256]{3,1,2,0:T(8,128)(2,1)}, bf16[1,2048,1,256]{3,1,2,0:T(8,128)(2,1)}, u32[]{:S(2)}, u32[]{:S(2)}) collective-permute-start(bf16[1,2048,1,256]{3,1,2,0:T(8,128)(2,1)} %get-tuple-element.1294), channel_id=1, source_target_pairs={{0,1},{1,2},{2,3},{3,4},{4,5},{5,6},{6,7},{7,8},{8,9},{9,10},{10,1... | collective-permute-start | bytes 3145736 | tf_op jit(solution)/shard_map/while/body/eval_jaxpr/ppermute | solution.py:61
  466.2 88.1 %collective-permute-start.1 = (bf16[1,2048,1,256]{1,3,2,0:T(8,128)(2,1)}, bf16[1,2048,1,256]{1,3,2,0:T(8,128)(2,1)S(1)}, u32[]{:S(2)}, u32[]{:S(2)}) collective-permute-start(bf16[1,2048,1,256]{1,3,2,0:T(8,128)(2,1)} %get-tuple-element.1295), channel_id=1, source_target_pairs={{0,1},{1,2},{2,3},{3,4},{4,5},{5,6},{6,7},{7,8},{8,9},{9,10},{10,1... | collective-permute-start | bytes 3145736 | tf_op jit(solution)/shard_map/while/body/eval_jaxpr/ppermute | solution.py:61
  468.3 91.4 %collective-permute-start.4 = (f32[1,1,2,2048]{3,2,1,0:T(2,128)S(1)}, f32[1,1,2,2048]{3,2,1,0:T(2,128)S(1)}, u32[]{:S(2)}, u32[]{:S(2)}) collective-permute-start(f32[1,1,2,2048]{3,2,1,0:T(2,128)S(1)} %get-tuple-element.1301), channel_id=1, source_target_pairs={{0,1},{1,2},{2,3},{3,4},{4,5},{5,6},{6,7},{7,8},{8,9},{9,10},{10,1... | collective-permute-start | bytes 49160 | tf_op jit(solution)/shard_map/while/body/eval_jaxpr/ppermute | solution.py:63
  628.5 107.3 %collective-permute-start.3 = (f32[1,2048,1,2,256]{4,3,2,1,0:T(2,128)}, f32[1,2048,1,2,256]{4,3,2,1,0:T(2,128)}, u32[]{:S(2)}, u32[]{:S(2)}) collective-permute-start(f32[1,2048,1,2,256]{4,3,2,1,0:T(2,128)} %get-tuple-element.1300), channel_id=1, source_target_pairs={{0,1},{1,2},{2,3},{3,4},{4,5},{5,6},{6,7},{7,8},{8,9},{9,10},{10,1... | collective-permute-start | bytes 12582920 | tf_op jit(solution)/shard_map/while/body/eval_jaxpr/ppermute | solution.py:63
  631.0 91.4 %collective-permute-start.2 = (bf16[1,2048,1,2,256]{4,3,2,1,0:T(2,128)(2,1)}, bf16[1,2048,1,2,256]{4,3,2,1,0:T(2,128)(2,1)}, u32[]{:S(2)}, u32[]{:S(2)}) collective-permute-start(bf16[1,2048,1,2,256]{4,3,2,1,0:T(2,128)(2,1)} %get-tuple-element.1296), channel_id=1, source_target_pairs={{0,1},{1,2},{2,3},{3,4},{4,5},{5,6},{6,7},{7,8},{8,9},{9,10},{10,1... | collective-permute-start | bytes 6291464 | tf_op jit(solution)/shard_map/while/body/eval_jaxpr/ppermute | solution.py:62
  631.1 79.1 %collective-permute-start = (bf16[1,2048,1,256]{3,1,2,0:T(8,128)(2,1)}, bf16[1,2048,1,256]{3,1,2,0:T(8,128)(2,1)}, u32[]{:S(2)}, u32[]{:S(2)}) collective-permute-start(bf16[1,2048,1,256]{3,1,2,0:T(8,128)(2,1)} %get-tuple-element.1294), channel_id=1, source_target_pairs={{0,1},{1,2},{2,3},{3,4},{4,5},{5,6},{6,7},{7,8},{8,9},{9,10},{10,1... | collective-permute-start | bytes 3145736 | tf_op jit(solution)/shard_map/while/body/eval_jaxpr/ppermute | solution.py:61
  633.2 88.1 %collective-permute-start.1 = (bf16[1,2048,1,256]{1,3,2,0:T(8,128)(2,1)}, bf16[1,2048,1,256]{1,3,2,0:T(8,128)(2,1)S(1)}, u32[]{:S(2)}, u32[]{:S(2)}) collective-permute-start(bf16[1,2048,1,256]{1,3,2,0:T(8,128)(2,1)} %get-tuple-element.1295), channel_id=1, source_target_pairs={{0,1},{1,2},{2,3},{3,4},{4,5},{5,6},{6,7},{7,8},{8,9},{9,10},{10,1... | collective-permute-start | bytes 3145736 | tf_op jit(solution)/shard_map/while/body/eval_jaxpr/ppermute | solution.py:61
  636.6 90.2 %collective-permute-start.4 = (f32[1,1,2,2048]{3,2,1,0:T(2,128)S(1)}, f32[1,1,2,2048]{3,2,1,0:T(2,128)S(1)}, u32[]{:S(2)}, u32[]{:S(2)}) collective-permute-start(f32[1,1,2,2048]{3,2,1,0:T(2,128)S(1)} %get-tuple-element.1301), channel_id=1, source_target_pairs={{0,1},{1,2},{2,3},{3,4},{4,5},{5,6},{6,7},{7,8},{8,9},{9,10},{10,1... | collective-permute-start | bytes 49160 | tf_op jit(solution)/shard_map/while/body/eval_jaxpr/ppermute | solution.py:63
  710.2 25.6 %collective-permute-start.5 = (f32[1,1,2,2048]{3,2,1,0:T(2,128)S(1)}, f32[1,1,2,2048]{3,2,1,0:T(2,128)S(1)}, u32[]{:S(2)}, u32[]{:S(2)}) collective-permute-start(f32[1,1,2,2048]{3,2,1,0:T(2,128)S(1)} %get-tuple-element.1302), channel_id=1, source_target_pairs={{0,1},{1,2},{2,3},{3,4},{4,5},{5,6},{6,7},{7,8},{8,9},{9,10},{10,1... | collective-permute-start | bytes 49160 | tf_op jit(solution)/shard_map/while/body/eval_jaxpr/ppermute | solution.py:63
  816.0 99.6 %collective-permute-start.3 = (f32[1,2048,1,2,256]{4,3,2,1,0:T(2,128)}, f32[1,2048,1,2,256]{4,3,2,1,0:T(2,128)}, u32[]{:S(2)}, u32[]{:S(2)}) collective-permute-start(f32[1,2048,1,2,256]{4,3,2,1,0:T(2,128)} %get-tuple-element.1300), channel_id=1, source_target_pairs={{0,1},{1,2},{2,3},{3,4},{4,5},{5,6},{6,7},{7,8},{8,9},{9,10},{10,1... | collective-permute-start | bytes 12582920 | tf_op jit(solution)/shard_map/while/body/eval_jaxpr/ppermute | solution.py:63
  816.0 91.4 %collective-permute-start.2 = (bf16[1,2048,1,2,256]{4,3,2,1,0:T(2,128)(2,1)}, bf16[1,2048,1,2,256]{4,3,2,1,0:T(2,128)(2,1)}, u32[]{:S(2)}, u32[]{:S(2)}) collective-permute-start(bf16[1,2048,1,2,256]{4,3,2,1,0:T(2,128)(2,1)} %get-tuple-element.1296), channel_id=1, source_target_pairs={{0,1},{1,2},{2,3},{3,4},{4,5},{5,6},{6,7},{7,8},{8,9},{9,10},{10,1... | collective-permute-start | bytes 6291464 | tf_op jit(solution)/shard_map/while/body/eval_jaxpr/ppermute | solution.py:62
  816.1 79.1 %collective-permute-start = (bf16[1,2048,1,256]{3,1,2,0:T(8,128)(2,1)}, bf16[1,2048,1,256]{3,1,2,0:T(8,128)(2,1)}, u32[]{:S(2)}, u32[]{:S(2)}) collective-permute-start(bf16[1,2048,1,256]{3,1,2,0:T(8,128)(2,1)} %get-tuple-element.1294), channel_id=1, source_target_pairs={{0,1},{1,2},{2,3},{3,4},{4,5},{5,6},{6,7},{7,8},{8,9},{9,10},{10,1... | collective-permute-start | bytes 3145736 | tf_op jit(solution)/shard_map/while/body/eval_jaxpr/ppermute | solution.py:61
  816.2 90.2 %collective-permute-start.1 = (bf16[1,2048,1,256]{1,3,2,0:T(8,128)(2,1)}, bf16[1,2048,1,256]{1,3,2,0:T(8,128)(2,1)S(1)}, u32[]{:S(2)}, u32[]{:S(2)}) collective-permute-start(bf16[1,2048,1,256]{1,3,2,0:T(8,128)(2,1)} %get-tuple-element.1295), channel_id=1, source_target_pairs={{0,1},{1,2},{2,3},{3,4},{4,5},{5,6},{6,7},{7,8},{8,9},{9,10},{10,1... | collective-permute-start | bytes 3145736 | tf_op jit(solution)/shard_map/while/body/eval_jaxpr/ppermute | solution.py:61
  816.3 95.6 %collective-permute-start.4 = (f32[1,1,2,2048]{3,2,1,0:T(2,128)S(1)}, f32[1,1,2,2048]{3,2,1,0:T(2,128)S(1)}, u32[]{:S(2)}, u32[]{:S(2)}) collective-permute-start(f32[1,1,2,2048]{3,2,1,0:T(2,128)S(1)} %get-tuple-element.1301), channel_id=1, source_target_pairs={{0,1},{1,2},{2,3},{3,4},{4,5},{5,6},{6,7},{7,8},{8,9},{9,10},{10,1... | collective-permute-start | bytes 49160 | tf_op jit(solution)/shard_map/while/body/eval_jaxpr/ppermute | solution.py:63
  895.2 20.4 %collective-permute-start.5 = (f32[1,1,2,2048]{3,2,1,0:T(2,128)S(1)}, f32[1,1,2,2048]{3,2,1,0:T(2,128)S(1)}, u32[]{:S(2)}, u32[]{:S(2)}) collective-permute-start(f32[1,1,2,2048]{3,2,1,0:T(2,128)S(1)} %get-tuple-element.1302), channel_id=1, source_target_pairs={{0,1},{1,2},{2,3},{3,4},{4,5},{5,6},{6,7},{7,8},{8,9},{9,10},{10,1... | collective-permute-start | bytes 49160 | tf_op jit(solution)/shard_map/while/body/eval_jaxpr/ppermute | solution.py:63
  995.7 99.6 %collective-permute-start.3 = (f32[1,2048,1,2,256]{4,3,2,1,0:T(2,128)}, f32[1,2048,1,2,256]{4,3,2,1,0:T(2,128)}, u32[]{:S(2)}, u32[]{:S(2)}) collective-permute-start(f32[1,2048,1,2,256]{4,3,2,1,0:T(2,128)} %get-tuple-element.1300), channel_id=1, source_target_pairs={{0,1},{1,2},{2,3},{3,4},{4,5},{5,6},{6,7},{7,8},{8,9},{9,10},{10,1... | collective-permute-start | bytes 12582920 | tf_op jit(solution)/shard_map/while/body/eval_jaxpr/ppermute | solution.py:63
  995.8 91.4 %collective-permute-start.2 = (bf16[1,2048,1,2,256]{4,3,2,1,0:T(2,128)(2,1)}, bf16[1,2048,1,2,256]{4,3,2,1,0:T(2,128)(2,1)}, u32[]{:S(2)}, u32[]{:S(2)}) collective-permute-start(bf16[1,2048,1,2,256]{4,3,2,1,0:T(2,128)(2,1)} %get-tuple-element.1296), channel_id=1, source_target_pairs={{0,1},{1,2},{2,3},{3,4},{4,5},{5,6},{6,7},{7,8},{8,9},{9,10},{10,1... | collective-permute-start | bytes 6291464 | tf_op jit(solution)/shard_map/while/body/eval_jaxpr/ppermute | solution.py:62
  995.9 79.1 %collective-permute-start = (bf16[1,2048,1,256]{3,1,2,0:T(8,128)(2,1)}, bf16[1,2048,1,256]{3,1,2,0:T(8,128)(2,1)}, u32[]{:S(2)}, u32[]{:S(2)}) collective-permute-start(bf16[1,2048,1,256]{3,1,2,0:T(8,128)(2,1)} %get-tuple-element.1294), channel_id=1, source_target_pairs={{0,1},{1,2},{2,3},{3,4},{4,5},{5,6},{6,7},{7,8},{8,9},{9,10},{10,1... | collective-permute-start | bytes 3145736 | tf_op jit(solution)/shard_map/while/body/eval_jaxpr/ppermute | solution.py:61
  995.9 90.2 %collective-permute-start.1 = (bf16[1,2048,1,256]{1,3,2,0:T(8,128)(2,1)}, bf16[1,2048,1,256]{1,3,2,0:T(8,128)(2,1)S(1)}, u32[]{:S(2)}, u32[]{:S(2)}) collective-permute-start(bf16[1,2048,1,256]{1,3,2,0:T(8,128)(2,1)} %get-tuple-element.1295), channel_id=1, source_target_pairs={{0,1},{1,2},{2,3},{3,4},{4,5},{5,6},{6,7},{7,8},{8,9},{9,10},{10,1... | collective-permute-start | bytes 3145736 | tf_op jit(solution)/shard_map/while/body/eval_jaxpr/ppermute | solution.py:61
  996.0 95.6 %collective-permute-start.4 = (f32[1,1,2,2048]{3,2,1,0:T(2,128)S(1)}, f32[1,1,2,2048]{3,2,1,0:T(2,128)S(1)}, u32[]{:S(2)}, u32[]{:S(2)}) collective-permute-start(f32[1,1,2,2048]{3,2,1,0:T(2,128)S(1)} %get-tuple-element.1301), channel_id=1, source_target_pairs={{0,1},{1,2},{2,3},{3,4},{4,5},{5,6},{6,7},{7,8},{8,9},{9,10},{10,1... | collective-permute-start | bytes 49160 | tf_op jit(solution)/shard_map/while/body/eval_jaxpr/ppermute | solution.py:63
  1074.9 20.4 %collective-permute-start.5 = (f32[1,1,2,2048]{3,2,1,0:T(2,128)S(1)}, f32[1,1,2,2048]{3,2,1,0:T(2,128)S(1)}, u32[]{:S(2)}, u32[]{:S(2)}) collective-permute-start(f32[1,1,2,2048]{3,2,1,0:T(2,128)S(1)} %get-tuple-element.1302), channel_id=1, source_target_pairs={{0,1},{1,2},{2,3},{3,4},{4,5},{5,6},{6,7},{7,8},{8,9},{9,10},{10,1... | collective-permute-start | bytes 49160 | tf_op jit(solution)/shard_map/while/body/eval_jaxpr/ppermute | solution.py:63
  1175.5 99.6 %collective-permute-start.3 = (f32[1,2048,1,2,256]{4,3,2,1,0:T(2,128)}, f32[1,2048,1,2,256]{4,3,2,1,0:T(2,128)}, u32[]{:S(2)}, u32[]{:S(2)}) collective-permute-start(f32[1,2048,1,2,256]{4,3,2,1,0:T(2,128)} %get-tuple-element.1300), channel_id=1, source_target_pairs={{0,1},{1,2},{2,3},{3,4},{4,5},{5,6},{6,7},{7,8},{8,9},{9,10},{10,1... | collective-permute-start | bytes 12582920 | tf_op jit(solution)/shard_map/while/body/eval_jaxpr/ppermute | solution.py:63
  1175.6 91.4 %collective-permute-start.2 = (bf16[1,2048,1,2,256]{4,3,2,1,0:T(2,128)(2,1)}, bf16[1,2048,1,2,256]{4,3,2,1,0:T(2,128)(2,1)}, u32[]{:S(2)}, u32[]{:S(2)}) collective-permute-start(bf16[1,2048,1,2,256]{4,3,2,1,0:T(2,128)(2,1)} %get-tuple-element.1296), channel_id=1, source_target_pairs={{0,1},{1,2},{2,3},{3,4},{4,5},{5,6},{6,7},{7,8},{8,9},{9,10},{10,1... | collective-permute-start | bytes 6291464 | tf_op jit(solution)/shard_map/while/body/eval_jaxpr/ppermute | solution.py:62
  1175.6 79.1 %collective-permute-start = (bf16[1,2048,1,256]{3,1,2,0:T(8,128)(2,1)}, bf16[1,2048,1,256]{3,1,2,0:T(8,128)(2,1)}, u32[]{:S(2)}, u32[]{:S(2)}) collective-permute-start(bf16[1,2048,1,256]{3,1,2,0:T(8,128)(2,1)} %get-tuple-element.1294), channel_id=1, source_target_pairs={{0,1},{1,2},{2,3},{3,4},{4,5},{5,6},{6,7},{7,8},{8,9},{9,10},{10,1... | collective-permute-start | bytes 3145736 | tf_op jit(solution)/shard_map/while/body/eval_jaxpr/ppermute | solution.py:61
  1175.7 90.2 %collective-permute-start.1 = (bf16[1,2048,1,256]{1,3,2,0:T(8,128)(2,1)}, bf16[1,2048,1,256]{1,3,2,0:T(8,128)(2,1)S(1)}, u32[]{:S(2)}, u32[]{:S(2)}) collective-permute-start(bf16[1,2048,1,256]{1,3,2,0:T(8,128)(2,1)} %get-tuple-element.1295), channel_id=1, source_target_pairs={{0,1},{1,2},{2,3},{3,4},{4,5},{5,6},{6,7},{7,8},{8,9},{9,10},{10,1... | collective-permute-start | bytes 3145736 | tf_op jit(solution)/shard_map/while/body/eval_jaxpr/ppermute | solution.py:61
  1175.8 95.6 %collective-permute-start.4 = (f32[1,1,2,2048]{3,2,1,0:T(2,128)S(1)}, f32[1,1,2,2048]{3,2,1,0:T(2,128)S(1)}, u32[]{:S(2)}, u32[]{:S(2)}) collective-permute-start(f32[1,1,2,2048]{3,2,1,0:T(2,128)S(1)} %get-tuple-element.1301), channel_id=1, source_target_pairs={{0,1},{1,2},{2,3},{3,4},{4,5},{5,6},{6,7},{7,8},{8,9},{9,10},{10,1... | collective-permute-start | bytes 49160 | tf_op jit(solution)/shard_map/while/body/eval_jaxpr/ppermute | solution.py:63
  1254.7 20.4 %collective-permute-start.5 = (f32[1,1,2,2048]{3,2,1,0:T(2,128)S(1)}, f32[1,1,2,2048]{3,2,1,0:T(2,128)S(1)}, u32[]{:S(2)}, u32[]{:S(2)}) collective-permute-start(f32[1,1,2,2048]{3,2,1,0:T(2,128)S(1)} %get-tuple-element.1302), channel_id=1, source_target_pairs={{0,1},{1,2},{2,3},{3,4},{4,5},{5,6},{6,7},{7,8},{8,9},{9,10},{10,1... | collective-permute-start | bytes 49160 | tf_op jit(solution)/shard_map/while/body/eval_jaxpr/ppermute | solution.py:63
  1355.2 99.6 %collective-permute-start.3 = (f32[1,2048,1,2,256]{4,3,2,1,0:T(2,128)}, f32[1,2048,1,2,256]{4,3,2,1,0:T(2,128)}, u32[]{:S(2)}, u32[]{:S(2)}) collective-permute-start(f32[1,2048,1,2,256]{4,3,2,1,0:T(2,128)} %get-tuple-element.1300), channel_id=1, source_target_pairs={{0,1},{1,2},{2,3},{3,4},{4,5},{5,6},{6,7},{7,8},{8,9},{9,10},{10,1... | collective-permute-start | bytes 12582920 | tf_op jit(solution)/shard_map/while/body/eval_jaxpr/ppermute | solution.py:63
  1355.3 91.4 %collective-permute-start.2 = (bf16[1,2048,1,2,256]{4,3,2,1,0:T(2,128)(2,1)}, bf16[1,2048,1,2,256]{4,3,2,1,0:T(2,128)(2,1)}, u32[]{:S(2)}, u32[]{:S(2)}) collective-permute-start(bf16[1,2048,1,2,256]{4,3,2,1,0:T(2,128)(2,1)} %get-tuple-element.1296), channel_id=1, source_target_pairs={{0,1},{1,2},{2,3},{3,4},{4,5},{5,6},{6,7},{7,8},{8,9},{9,10},{10,1... | collective-permute-start | bytes 6291464 | tf_op jit(solution)/shard_map/while/body/eval_jaxpr/ppermute | solution.py:62
  1355.4 79.1 %collective-permute-start = (bf16[1,2048,1,256]{3,1,2,0:T(8,128)(2,1)}, bf16[1,2048,1,256]{3,1,2,0:T(8,128)(2,1)}, u32[]{:S(2)}, u32[]{:S(2)}) collective-permute-start(bf16[1,2048,1,256]{3,1,2,0:T(8,128)(2,1)} %get-tuple-element.1294), channel_id=1, source_target_pairs={{0,1},{1,2},{2,3},{3,4},{4,5},{5,6},{6,7},{7,8},{8,9},{9,10},{10,1... | collective-permute-start | bytes 3145736 | tf_op jit(solution)/shard_map/while/body/eval_jaxpr/ppermute | solution.py:61
  1355.5 90.2 %collective-permute-start.1 = (bf16[1,2048,1,256]{1,3,2,0:T(8,128)(2,1)}, bf16[1,2048,1,256]{1,3,2,0:T(8,128)(2,1)S(1)}, u32[]{:S(2)}, u32[]{:S(2)}) collective-permute-start(bf16[1,2048,1,256]{1,3,2,0:T(8,128)(2,1)} %get-tuple-element.1295), channel_id=1, source_target_pairs={{0,1},{1,2},{2,3},{3,4},{4,5},{5,6},{6,7},{7,8},{8,9},{9,10},{10,1... | collective-permute-start | bytes 3145736 | tf_op jit(solution)/shard_map/while/body/eval_jaxpr/ppermute | solution.py:61
  1355.5 95.6 %collective-permute-start.4 = (f32[1,1,2,2048]{3,2,1,0:T(2,128)S(1)}, f32[1,1,2,2048]{3,2,1,0:T(2,128)S(1)}, u32[]{:S(2)}, u32[]{:S(2)}) collective-permute-start(f32[1,1,2,2048]{3,2,1,0:T(2,128)S(1)} %get-tuple-element.1301), channel_id=1, source_target_pairs={{0,1},{1,2},{2,3},{3,4},{4,5},{5,6},{6,7},{7,8},{8,9},{9,10},{10,1... | collective-permute-start | bytes 49160 | tf_op jit(solution)/shard_map/while/body/eval_jaxpr/ppermute | solution.py:63
  1434.4 20.4 %collective-permute-start.5 = (f32[1,1,2,2048]{3,2,1,0:T(2,128)S(1)}, f32[1,1,2,2048]{3,2,1,0:T(2,128)S(1)}, u32[]{:S(2)}, u32[]{:S(2)}) collective-permute-start(f32[1,1,2,2048]{3,2,1,0:T(2,128)S(1)} %get-tuple-element.1302), channel_id=1, source_target_pairs={{0,1},{1,2},{2,3},{3,4},{4,5},{5,6},{6,7},{7,8},{8,9},{9,10},{10,1... | collective-permute-start | bytes 49160 | tf_op jit(solution)/shard_map/while/body/eval_jaxpr/ppermute | solution.py:63
  1460.3 228.3 %collective-permute-start.7 = (f32[1,2048,1,2,256]{4,3,1,2,0:T(2,128)}, f32[1,2048,1,2,256]{4,3,1,2,0:T(2,128)}, u32[]{:S(2)}, u32[]{:S(2)}) collective-permute-start(f32[1,2048,1,2,256]{4,3,1,2,0:T(2,128)} %bitcast.221), channel_id=1, source_target_pairs={{0,8},{1,9},{2,10},{3,11},{4,12},{5,13},{6,14},{7,15},{8,0},{9,1},... | collective-permute-start | bytes 12582920 | tf_op jit(solution)/shard_map/ppermute | solution.py:81
  1511.6 175.7 %collective-permute-start.6 = (f32[1,1,2,2048]{3,2,1,0:T(2,128)S(1)}, f32[1,1,2,2048]{3,2,1,0:T(2,128)S(1)}, u32[]{:S(2)}, u32[]{:S(2)}) collective-permute-start(f32[1,1,2,2048]{3,2,1,0:T(2,128)S(1)} %get-tuple-element.721), channel_id=1, source_target_pairs={{0,8},{1,9},{2,10},{3,11},{4,12},{5,13},{6,14},{7,15},{8,0},{9,1},... | collective-permute-start | bytes 49160 | tf_op jit(solution)/shard_map/ppermute | solution.py:81
  1511.8 175.7 %collective-permute-start.8 = (f32[1,1,2,2048]{3,2,1,0:T(2,128)S(1)}, f32[1,1,2,2048]{3,2,1,0:T(2,128)S(1)}, u32[]{:S(2)}, u32[]{:S(2)}) collective-permute-start(f32[1,1,2,2048]{3,2,1,0:T(2,128)S(1)} %get-tuple-element.724), channel_id=1, source_target_pairs={{0,8},{1,9},{2,10},{3,11},{4,12},{5,13},{6,14},{7,15},{8,0},{9,1},... | collective-permute-start | bytes 49160 | tf_op jit(solution)/shard_map/ppermute | solution.py:81
  (91 other events, 1068.6 us)
where the time goes:
time: 1700 us
  waiting for transfers between devices  841 us (49%)
  matrix products  387 us (23%)
  local copies, waits for them, and re-layouts  269 us (16%)
  starting transfers between devices  118 us (7%)
  other arithmetic  80.1 us (5%)
    ppermute x16, waiting for transfers between devices, round_body(): kv_trav = lax.ppermute(kv_trav, 'ctx', next_perm)  653 us
    dot_general x64, matrix products, tile_update(): jnp.einsum('bhgqk,bkhd->bqhgd', exp_scores.astype(jnp.bfloat16), v_tile,...  258 us
    while x288, local copies, waits for them, and re-layouts  172 us
    ppermute x3, waiting for transfers between devices, local_attention(): acc_home = lax.ppermute(loop_state[3], 'ctx', home_perm)  163 us
    dot_general x64, matrix products, tile_update(): jnp.einsum('bqhgd,bkhd->bhgqk', q_blk, k_tile, preferred_element_type=jnp...  129 us
    another operation x15, local copies, waits for them, and re-layouts  68.8 us
    reduce_sum x64, other arithmetic, tile_update(): l_new = l_acc * rescale + jnp.sum(exp_scores, axis=-1)  63.9 us
    ppermute x3, starting transfers between devices, local_attention(): acc_home = lax.ppermute(loop_state[3], 'ctx', home_perm)  56.7 us
  transfers between devices with their start and end apart: 51, of which 23 were waited for; matrix products, arithmetic and copies ran while one was open for 4% of the time, Pallas kernels for 0%

commit v1 on v0

v1 whole, which is shorter than its diff:
```python
import functools
import math

import jax
import jax.numpy as jnp
from jax import lax
from jax.experimental import pallas as pl
from jax.experimental.pallas import tpu as pltpu
from jax.sharding import PartitionSpec as P

MESH = pl.DeviceIdType.MESH
CP = 8
NT = (((1,), (1,)), ((), ()))
NN = (((1,), (0,)), ((), ()))


def kernel(n, scale2, q_hbm, k_hbm, v_hbm, out_hbm,
           kv, qraw, q_s, oraw, acc, m_s, l_s, s_s, mx_s, vt_s,
           load_sem, qload_sem, recv_sem, qrecv_sem, orecv_sem, ostore_sem,
           up_sem, dn_sem, sib_sem, qsend_sem, osend_sem):
    me = lax.axis_index("ctx")
    chip, core = me // 2, me % 2
    sib = 1 - core
    half = n // 2
    n_pos = CP * (n - 1) // 2
    own0 = n_pos
    ch = k_hbm.shape[1]
    d = k_hbm.shape[2]
    rows = q_s.shape[1]
    gk = 4 * ch

    def dev(c, k):
        return {"ctx": c * 2 + k}

    sib_dev = dev(chip, sib)
    above = lax.rem(chip + 1, n)
    below = lax.rem(chip + n - 1, n)
    up_dev, dn_dev = dev(above, core), dev(below, core)
    low = chip < half

    def up_count(c):
        return jnp.where(c < half, c * CP, c * (CP // 2))

    def up_slot(c, u):
        lo = c < half
        return jnp.where(lo, u // 2, u), jnp.where(lo, 2 * (u % 2) + core, core)

    n_up = up_count(chip)
    n_up_above = jnp.where(chip + 1 < n, up_count(chip + 1), 0)
    n_dn = jnp.where(low, 0, chip * (CP // 2))
    n_dn_below = jnp.where(chip - 1 < half, 0, (chip - 1) * (CP // 2))
    n_steps = chip * (CP // 2)
    transit0 = CP * (chip + 1)
    n_transit = jnp.where(low, jnp.maximum(n_pos - transit0, 0), 0)

    def own_chunk(j):
        jj = core * CP + j
        return own0 + jj // 4, jj % 4

    def sib_chunk(j):
        jj = sib * CP + j
        return own0 + jj // 4, jj % 4

    def block_row(j):
        return 2 * j + lax.rem(core + j, 2)

    def send(slot_from, slot_to, sem, device):
        return pltpu.make_async_remote_copy(
            src_ref=kv.at[slot_from[0], slot_from[1]], dst_ref=kv.at[slot_to[0], slot_to[1]],
            send_sem=sem, recv_sem=recv_sem.at[slot_to[0], slot_to[1]],
            device_id=device, device_id_type=MESH)

    def arrived(slot):
        send(slot, slot, sib_sem, sib_dev).wait_recv()

    loads = []
    for j in range(CP):
        a, b = own_chunk(j)
        loads.append((pltpu.make_async_copy(k_hbm.at[j], kv.at[a, b, 0], load_sem.at[j, 0]),
                      pltpu.make_async_copy(v_hbm.at[j], kv.at[a, b, 1], load_sem.at[j, 1])))
    for j in reversed(range(CP)):
        loads[j][0].start()
        loads[j][1].start()
    qloads = []
    for i in range(CP // 2):
        j = core * (CP // 2) + i
        qloads.append(pltpu.make_async_copy(q_hbm.at[block_row(j) - core * CP], qraw.at[j], qload_sem.at[i]))
        qloads[-1].start()

    barrier = pltpu.get_barrier_semaphore()
    for device in (sib_dev, up_dev, dn_dev):
        pl.semaphore_signal(barrier, inc=1, device_id=device, device_id_type=MESH)
    pl.semaphore_wait(barrier, 3)

    def q_give(i):
        j = core * (CP // 2) + i
        row = 2 * j + lax.rem(sib + j, 2) - core * CP
        return pltpu.make_async_remote_copy(
            src_ref=q_hbm.at[row], dst_ref=qraw.at[j], send_sem=qsend_sem.at[i], recv_sem=qrecv_sem.at[i],
            device_id=sib_dev, device_id_type=MESH)

    def q_take(i):
        j = sib * (CP // 2) + i
        return pltpu.make_async_remote_copy(
            src_ref=q_hbm.at[0], dst_ref=qraw.at[j], send_sem=qsend_sem.at[i], recv_sem=qrecv_sem.at[i],
            device_id=sib_dev, device_id_type=MESH)

    for u in range(CP):
        j = CP - 1 - u
        loads[j][0].wait()
        loads[j][1].wait()

        @pl.when(u < n_up_above)
        def _():
            send(own_chunk(j), up_slot(chip + 1, u), up_sem, up_dev).start()

    first_dn = chip * CP
    for j in range(CP):
        @pl.when(first_dn + j < n_pos)
        def _():
            send(own_chunk(j), (first_dn + j, 2 + core), dn_sem, dn_dev).start()
    for i in range(CP // 2):
        q_give(i).start()
    for j in range(CP):
        send(own_chunk(j), own_chunk(j), sib_sem, sib_dev).start()

    def serve_up(p):
        @pl.when(p < n_up)
        def _():
            slot = up_slot(chip, p)
            arrived(slot)

            @pl.when(p + CP < n_up_above)
            def _():
                send(slot, up_slot(chip + 1, p + CP), up_sem, up_dev).start()
            send(slot, slot, sib_sem, sib_dev).start()

    def serve_dn(p):
        @pl.when(p < n_dn)
        def _():
            slot = (p, 2 + core)
            arrived(slot)

            @pl.when(p < n_dn_below)
            def _():
                send(slot, slot, dn_sem, dn_dev).start()
            send(slot, slot, sib_sem, sib_dev).start()

    def serve_transit(p):
        @pl.when(p < n_transit)
        def _():
            slot = (transit0 + p, 2 + core)
            arrived(slot)
            send(slot, slot, dn_sem, dn_dev).start()

    def serve(s):
        @pl.when(low)
        def _():
            for i in range(2):
                serve_transit(2 * s + i)
            for i in range(2):
                serve_up(2 * s + i)

        @pl.when(jnp.logical_not(low))
        def _():
            serve_up(s)
            serve_dn(s)

    def wait_sibling(s):
        @pl.when(s < n_steps)
        def _():
            arrived((s, sib))
            arrived((s, 2 + sib))

    def qk(j, g, c0, nk, slot, off):
        k = kv[g, c0:c0 + nk // ch, 0].reshape(nk, d)
        s = lax.dot_general(k, q_s[j], NT, preferred_element_type=jnp.float32)
        if off is not None:
            key = lax.broadcasted_iota(jnp.int32, (nk, rows), 0)
            tok = lax.broadcasted_iota(jnp.int32, (nk, rows), 1) // 2
            s = jnp.where(key - tok <= off, s, -jnp.inf)
        s_s[slot, 0:nk] = s
        mx_s[slot] = jnp.max(s.reshape(nk // 8, 8, rows), axis=0)

    def sm_pv(j, v, c0, nk, slot):
        m_old = m_s[j]
        m_new = jnp.maximum(m_old, jnp.max(mx_s[slot], axis=0, keepdims=True))
        alpha = jnp.exp2((m_old - m_new) * scale2)
        m_s[j] = m_new
        p = jnp.exp2((s_s[slot, 0:nk].reshape(nk // 8, 8, rows) - m_new[None]) * scale2)
        l_s[j] = l_s[j] * alpha + jnp.sum(p, axis=0)
        pv = lax.dot_general(vt_s[v, :, c0 * ch:c0 * ch + nk], p.reshape(nk, rows).astype(jnp.bfloat16), NN,
                             preferred_element_type=jnp.float32)
        acc[j] = (acc[j].reshape(d // 8, 8, rows) * alpha[None]).reshape(d, rows) + pv

    def make_vt(g, v):
        vt_s[v] = kv[g, :, 1].reshape(gk, d).T

    def run(tiles, nxt=None):
        for t, (j, g, c0, nk, off, v) in enumerate(tiles):
            if t + 1 < len(tiles):
                j1, g1, c1, nk1, off1, _ = tiles[t + 1]
                qk(j1, g1, c1, nk1, (t + 1) % 2, off1)
            elif nxt is not None:
                qk(0, nxt, 0, gk, (t + 1) % 2, None)
            sm_pv(j, v, c0, nk, t % 2)

    m_s[...] = jnp.full_like(m_s, -jnp.inf)
    l_s[...] = jnp.zeros_like(l_s)
    acc[...] = jnp.zeros_like(acc)

    def triangle(h):
        for i in range(CP // 2):
            j = h * (CP // 2) + i
            q_s[j] = qraw[j].reshape(rows, d)
        tiles = []
        off_even = ch * core
        off_odd = ch * (3 - core)
        for e in range(2):
            make_vt(own0 + 2 * h + e, e)
        for i in range(CP // 2):
            j = h * (CP // 2) + i
            for e in range(i // 2):
                tiles.append((j, own0 + 2 * h + e, 0, gk, None, e))
            e = i // 2
            if i % 2 == 0:
                tiles.append((j, own0 + 2 * h + e, 0, 2 * ch, off_even, e))
            else:
                tiles.append((j, own0 + 2 * h + e, 0, gk, off_odd, e))
        qk(tiles[0][0], tiles[0][1], tiles[0][2], tiles[0][3], 0, tiles[0][4])
        run(tiles)

    def both_triangles(r, carry):
        h = lax.rem(core + r, 2)

        @pl.when(r == 0)
        def _():
            for cp in qloads:
                cp.wait()

        @pl.when(r == 1)
        def _():
            for i in range(CP // 2):
                q_take(i).wait_recv()
            for j in range(CP):
                arrived(sib_chunk(j))
        triangle(h)
        return carry

    lax.fori_loop(0, 2, both_triangles, 0)
    serve(0)

    def next_group(s):
        return jnp.where(s < n_steps, s, own0)

    for e in range(2):
        make_vt(own0 + e, e)
    tiles = [(j, own0 + e, 0, gk, None, e) for e in range(2) for j in range(CP // 2, CP)]
    qk(tiles[0][0], tiles[0][1], 0, gk, 0, None)
    run(tiles[:-1], None)
    wait_sibling(0)
    g0 = next_group(0)
    qk(tiles[-1][0], tiles[-1][1], 0, gk, 1, None)
    qk(0, g0, 0, gk, 0, None)
    sm_pv(tiles[-1][0], 1, 0, gk, 1)
    make_vt(g0, 0)

    def step(s, carry):
        v = lax.rem(s, 2)
        t = lambda j: (j, s, 0, gk, None, v)
        for j in range(4):
            qk(j + 1, s, 0, gk, (j + 1) % 2, None)
            sm_pv(j, v, 0, gk, j % 2)
        serve(s + 1)
        for j in range(4, CP - 1):
            qk(j + 1, s, 0, gk, (j + 1) % 2, None)
            sm_pv(j, v, 0, gk, j % 2)
        wait_sibling(s + 1)
        g = next_group(s + 1)
        qk(0, g, 0, gk, 0, None)
        make_vt(g, 1 - v)
        sm_pv(CP - 1, v, 0, gk, 1)
        return carry

    lax.fori_loop(0, n_steps, step, 0)

    n_serve = jnp.maximum(n_steps, (n_transit + 1) // 2)

    def rest(s, carry):
        serve(s + 1)
        return carry

    lax.fori_loop(n_steps, n_serve, rest, 0)

    def o_home(i):
        j = core * (CP // 2) + i
        return pltpu.make_async_copy(oraw.at[j], out_hbm.at[block_row(j) - core * CP], ostore_sem.at[i])

    def o_give(i):
        j = sib * (CP // 2) + i
        return pltpu.make_async_remote_copy(
            src_ref=oraw.at[j], dst_ref=out_hbm.at[block_row(j) - sib * CP], send_sem=osend_sem.at[i],
            recv_sem=orecv_sem.at[i], device_id=sib_dev, device_id_type=MESH)

    def o_take(i):
        j = core * (CP // 2) + i
        row = 2 * j + lax.rem(sib + j, 2) - core * CP
        return pltpu.make_async_remote_copy(
            src_ref=oraw.at[j], dst_ref=out_hbm.at[row], send_sem=osend_sem.at[i],
            recv_sem=orecv_sem.at[i], device_id=sib_dev, device_id_type=MESH)

    def finish(j):
        inv = 1.0 / jnp.sum(l_s[j], axis=0, keepdims=True)
        o = acc[j] * inv
        oraw[j] = o.T.astype(jnp.bfloat16).reshape(ch, rows // ch, d)

    for i in range(CP // 2):
        finish(sib * (CP // 2) + i)
        o_give(i).start()
    for i in range(CP // 2):
        finish(core * (CP // 2) + i)
        o_home(i).start()

    def drain(count, sem):
        def one(i, carry):
            send((own0, 0), (own0, 0), sem, sib_dev).wait_send()
            return carry
        lax.fori_loop(0, count, one, 0)

    own_up = jnp.minimum(n_up_above, CP)
    own_dn = jnp.clip(n_pos - first_dn, 0, CP)
    drain(own_up + jnp.clip(n_up_above - CP, 0, n_up), up_sem)
    drain(own_dn + n_dn_below + n_transit, dn_sem)
    drain(CP + n_up + n_dn, sib_sem)
    for i in range(CP // 2):
        q_give(i).wait_send()
        o_give(i).wait_send()
        o_home(i).wait()
        o_take(i).wait_recv()


def solution(mesh):
    n = mesh.shape["ctx"] // 2
    seq_spec = P("data", "ctx", None, None)

    def local_attention(queries, key_rows, value_rows):
        n_batch, chunk_len, n_heads, head_dim = queries.shape
        ch = chunk_len // CP
        rows = ch * n_heads
        n_pos = CP * (n - 1) // 2
        bf16, f32 = jnp.bfloat16, jnp.float32
        hbm = pl.BlockSpec(memory_space=pltpu.HBM)
        dma = pltpu.SemaphoreType.DMA
        out = pl.pallas_call(
            functools.partial(kernel, n, math.log2(math.e) / math.sqrt(head_dim)),
            out_shape=jax.ShapeDtypeStruct((CP, ch, n_heads, head_dim), bf16),
            in_specs=[hbm, hbm, hbm],
            out_specs=hbm,
            scratch_shapes=[
                pltpu.VMEM((n_pos + 4, 4, 2, ch, head_dim), bf16),
                pltpu.VMEM((CP, ch, n_heads, head_dim), bf16),
                pltpu.VMEM((CP, rows, head_dim), bf16),
                pltpu.VMEM((CP, ch, n_heads, head_dim), bf16),
                pltpu.VMEM((CP, head_dim, rows), f32),
                pltpu.VMEM((CP, 8, rows), f32),
                pltpu.VMEM((CP, 8, rows), f32),
                pltpu.VMEM((2, 4 * ch, rows), f32),
                pltpu.VMEM((2, 8, rows), f32),
                pltpu.VMEM((2, head_dim, 4 * ch), bf16),
                dma((CP, 2)), dma((CP // 2,)), dma((n_pos + 4, 4)), dma((CP // 2,)), dma((CP // 2,)), dma((CP // 2,)),
                dma, dma, dma, dma((CP // 2,)), dma((CP // 2,)),
            ],
            compiler_params=pltpu.CompilerParams(
                collective_id=0, has_side_effects=True, vmem_limit_bytes=60 * 1024 * 1024),
            name="attention",
        )(queries.reshape(CP, ch, n_heads, head_dim), key_rows.reshape(CP, ch, head_dim),
          value_rows.reshape(CP, ch, head_dim))
        return out.reshape(queries.shape)

    return jax.shard_map(local_attention, mesh=mesh, in_specs=(seq_spec, seq_spec, seq_spec),
                         out_specs=seq_spec, check_vma=False)
```

time: 1700 us -> 185 us (0.11)
  the two profiles are of different devices: /device:TPU:61 before, /device:TPU:247 now
where the time goes in v1:
time: 185 us
  Pallas kernels  180 us (97%)
  local copies, waits for them, and re-layouts  4.43 us (2%)
    pallas_call x1, Pallas kernels, local_attention(): pl.pallas_call(functools.partial(kernel, n, math.log2(math.e) / math.sqrt...  180 us
    unnamed x1, local copies, waits for them, and re-layouts  4.43 us

profile of v1, /device:TPU:247, one launch (start us, length us, event | category | flops | bytes accessed | tf_op | source)
XLA Modules:
  0.0 184.6 jit_solution(5960735019916150818)
XLA Ops:
  0.0 180.1 %attention.1 = bf16[8,256,2,256]{3,2,1,0:T(2,128)(2,1)} custom-call(bf16[8,256,2,256]{3,2,1,0:T(2,128)(2,1)} %bitcast.5, bf16[8,256,256]{2,1,0:T(8,128)(2,1)} %bitcast.6, bf16[8,256,256]{2,1,0:T(8,128)(2,1)} %bitcast.7), custom_call_target="tpu_custom_call" | custom-call | tf_op jit(solution)/shard_map/attention/pallas_call | solution.py:354
  180.1 4.4 %copy.5 = bf16[1,2048,2,256]{3,2,1,0:T(2,128)(2,1)} copy(bf16[1,2048,2,256]{3,2,1,0:T(2,128)(2,1)} %bitcast.4) | data formatting | bytes 4194304
